TPU v7x, 32 devices: a whole 2x2x4 slice. The times are simulated.
32 devices in a mesh: dp: 16 (over z, x, core), tensor: 2 (over y).
Axes of the slice: x: 2, y: 2, z: 4, core: 2. Of those that a mesh axis runs over, the one named last changes fastest.
Arguments:
- activations: bfloat16 [4096, 2880], P(('dp', 'tensor')), parts along dimension 0, may hold values from -6 to 6
- segment_ids: int32 [4096], P('dp'), parts along dimension 0, may hold values from 0 to 3, as said below
- attn_gain: float32 [2880], replicated, may hold values from 0.1 to 1.9
- qkv_weight: bfloat16 [2880, 5120], P(None, 'tensor'), may hold values from -2 to 2
- out_weight: bfloat16 [4096, 2880], P('tensor'), may hold values from -0.09375 to 0.09375
- ffn_gain: float32 [2880], replicated, may hold values from 0.1 to 1.9
- gate_weight: bfloat16 [2880, 2048], P(None, 'tensor'), may hold values from -0.109375 to 0.109375
- up_weight: bfloat16 [2880, 2048], P(None, 'tensor'), may hold values from -0.109375 to 0.109375
- down_weight: bfloat16 [2048, 2880], P('tensor'), may hold values from -0.125 to 0.125
Outputs:
- layer_out: bfloat16 [4096, 2880], P(('dp', 'tensor')), parts along dimension 0
There are 16 independent parts, one for each index of `dp`. A program takes and returns all parts, laid end to end along the dimension named above; an argument that names none is the same for every part. Nothing has to cross between parts.
Inputs may be any that keep to these rules, and one draw needn't show every extreme that they name: `segment_ids`: segment numbers never fall along the tokens, and each of the four segments holds at least one token.
All inputs are finite; a program needn't handle non-finite values.
Results may differ from a plain program's by a relative error of at most 0.035.
Values may be sent and summed in bfloat16 or wider, within the bound.
No kernel may reach another device: no remote copies, remote signals or barrier semaphores. Data moves between devices by JAX's collectives and lax.ppermute only.
A program may use at most 128 MiB of HBM per device.

v0:
```python
import jax
import jax.numpy as jnp
from jax import lax
from jax.sharding import PartitionSpec as P

HEADS = 64
KV_HEADS = 8
HEAD_DIM = 64


def normalize(rows_in, gain):
    floats = rows_in.astype(jnp.float32)
    mean_square = jnp.mean(floats * floats, axis=-1, keepdims=True)
    return (floats * lax.rsqrt(mean_square + 1e-05) * gain).astype(jnp.bfloat16)


def attend(projected, segment_ids):
    token_count = projected.shape[0]
    group_size = HEADS // KV_HEADS
    heads_view = projected.reshape(token_count, -1, group_size + 2, HEAD_DIM)
    key_rows = heads_view[:, :, group_size]
    value_rows = heads_view[:, :, group_size + 1]
    block_rows = token_count if token_count <= 512 else 512
    block_count = token_count // block_rows
    positions = jnp.arange(token_count, dtype=jnp.int32)

    def one_block(block_index):
        first_row = block_index * block_rows
        query_rows = lax.dynamic_slice_in_dim(heads_view, first_row, block_rows, 0)[
            :, :, :group_size
        ]
        query_pos = first_row + jnp.arange(block_rows, dtype=jnp.int32)
        query_seg = lax.dynamic_slice_in_dim(segment_ids, first_row, block_rows, 0)
        scores = jnp.einsum(
            "sngd,tnd->ngst", query_rows, key_rows, preferred_element_type=jnp.float32
        ) * HEAD_DIM ** (-0.5)
        allowed = (positions[None, :] <= query_pos[:, None]) & (
            segment_ids[None, :] == query_seg[:, None]
        )
        scores = jnp.where(allowed, scores, -1e30)
        row_max = jnp.max(scores, axis=-1, keepdims=True)
        weights = jnp.exp(scores - row_max)
        row_total = jnp.sum(weights, axis=-1, keepdims=True)
        softmax_out = (weights / row_total).astype(jnp.bfloat16)
        mixed = jnp.einsum(
            "ngst,tnd->sngd", softmax_out, value_rows, preferred_element_type=jnp.float32
        )
        return mixed.astype(jnp.bfloat16)

    blocks_out = lax.map(one_block, jnp.arange(block_count, dtype=jnp.int32))
    return blocks_out.reshape(token_count, -1)


def shards(
    activations,
    segment_ids,
    attn_gain,
    qkv_weight,
    out_weight,
    ffn_gain,
    gate_weight,
    up_weight,
    down_weight,
):
    own_rows = activations.shape[0]
    whole_rows = lax.all_gather(activations, "tensor", axis=0, tiled=True)
    projected = jnp.dot(
        normalize(whole_rows, attn_gain), qkv_weight, preferred_element_type=jnp.float32
    ).astype(jnp.bfloat16)
    mixed_heads = attend(projected, segment_ids)
    head_total = lax.psum(
        jnp.dot(mixed_heads, out_weight, preferred_element_type=jnp.float32).astype(jnp.bfloat16),
        "tensor",
    ).astype(jnp.float32)
    resid_whole = (whole_rows.astype(jnp.float32) + head_total).astype(jnp.bfloat16)
    shard_rows = normalize(resid_whole, ffn_gain)
    gate_act = jnp.dot(shard_rows, gate_weight, preferred_element_type=jnp.float32)
    up_act = jnp.dot(shard_rows, up_weight, preferred_element_type=jnp.float32)
    hidden = (jax.nn.silu(gate_act) * up_act).astype(jnp.bfloat16)
    resid_sum = lax.dynamic_slice_in_dim(
        resid_whole, lax.axis_index("tensor") * own_rows, own_rows, 0
    )
    ffn_out = lax.psum_scatter(
        jnp.dot(hidden, down_weight, preferred_element_type=jnp.float32).astype(jnp.bfloat16),
        "tensor",
        scatter_dimension=0,
        tiled=True,
    ).astype(jnp.float32)
    return (resid_sum.astype(jnp.float32) + ffn_out).astype(jnp.bfloat16)


def solution(mesh):
    placed = (
        P(("dp", "tensor"), None),
        P("dp"),
        P(),
        P(None, "tensor"),
        P("tensor", None),
        P(),
        P(None, "tensor"),
        P(None, "tensor"),
        P("tensor", None),
    )
    return jax.shard_map(
        shards, mesh=mesh, in_specs=placed, out_specs=P(("dp", "tensor"), None), check_vma=False
    )
```

profile of v0, /device:TPU:0, one launch (start us, length us, event | category | flops | bytes accessed | tf_op | source)
XLA Modules:
  0.0 167.5 jit_solution(3976080794666431789)
XLA Ops:
  6.5 0.0 all-gather.2.cloned.1.call-start
  6.5 0.7 all-gather.2.cloned.1.call-update
  7.3 0.0 all-reduce.2.cloned.1.call-start
  7.3 0.9 fusion.25
  8.2 29.5 %all-gather.2.cloned.1.call-done = bf16[256,2880]{0,1:T(8,128)(2,1)} async-done(((bf16[128,2880]{0,1:T(8,128)(2,1)}), bf16[256,2880]{0,1:T(8,128)(2,1)}) %all-gather.2.cloned.1.call-update) | async-done | bytes 1474576 | tf_op jit(solution)/shard_map/all_gather | solution.py:66
  37.7 1.8 %fusion.9 = f32[256]{0:T(256)S(1)} fusion(bf16[256,2880]{0,1:T(8,128)(2,1)} %all-gather.2.cloned.1.call-done), kind=kLoop, calls=%fused_computation.20 | loop fusion | flops 2211584 | bytes 1475584 | tf_op jit(solution)/shard_map/reduce_sum | solution.py:13
  39.5 10.0 %convolution_convert_fusion.2 = bf16[256,2560]{1,0:T(8,128)(2,1)S(1)} fusion(bf16[2880,2560]{1,0:T(8,128)(2,1)} %param.12, bf16[256,2880]{0,1:T(8,128)(2,1)} %all-gather.2.cloned.1.call-done, f32[2880]{0:T(1024)} %param.11, f32[256]{0:T(256)S(1)} %add_rsqrt_fusion.1), kind=kOutput, calls=%fused_computation.14 | convolution fusion | flops 3778478080 | bytes 17543424 | tf_op jit(solution)/shard_map/dot_general | solution.py:67
  49.5 0.6 copy.18
  50.1 1.3 fusion.18
  51.4 0.0 slice-start
  51.4 0.0 slice-start.1
  51.4 5.1 %fusion.30 = (f32[4,8,256]{2,1,0:T(8,128)S(1)}, f32[4,8,256,256]{2,3,1,0:T(8,128)}) fusion(f32[4,256,256,8]{2,1,3,0:T(8,128)S(1)} %fusion.18, pred[256,256]{0,1:T(8,128)(4,1)S(1)} %fusion.25), kind=kOutput, calls=%fused_computation.43 | output fusion | flops 12583167 | bytes 16875520 | tf_op jit(solution)/shard_map/while/body/eval_jaxpr/sub | solution.py:42
  56.5 0.0 slice-start.2
  56.5 4.4 %fusion.13 = bf16[4,64,8,256]{3,1,2,0:T(8,128)(2,1)S(1)} fusion(f32[4,8,256,256]{2,3,1,0:T(8,128)} %get-tuple-element.20, f32[4,8,256]{2,1,0:T(8,128)S(1)} %get-tuple-element.19, bf16[256,4,10,64]{0,3,2,1:T(8,128)(2,1)S(1)} %bitcast.39), kind=kOutput, calls=%fused_computation.24 | convolution fusion | flops 273154048 | bytes 9601024 | tf_op jit(solution)/shard_map/while/body/eval_jaxpr/ngst,tnd->sngd/dot_general | solution.py:45
  60.9 0.0 slice-done
  60.9 0.0 slice-done.1
  60.9 0.3 slice-done.2
  61.2 0.0 copy-start
  61.2 4.3 %convolution_convert_fusion = bf16[256,2880]{0,1:T(8,128)(2,1)} fusion(bf16[2048,2880]{0,1:T(8,128)(2,1)S(1)} %bitcast.41, bf16[256,2048]{0,1:T(8,128)(2,1)S(1)} %bitcast.42), kind=kOutput, calls=%fused_computation.12 | convolution fusion | flops 3020636160 | bytes 14319616 | tf_op jit(solution)/shard_map/dot_general | solution.py:72
  65.6 0.0 copy-start.1
  65.6 0.0 all-reduce.2.cloned.1.call-update
  65.6 0.2 reduce-scatter.4.cloned.1.call-start
  65.8 49.3 %all-reduce.2.cloned.1.call-done = bf16[256,2880]{0,1:T(8,128)(2,1)} async-done(((bf16[256,2880]{0,1:T(8,128)(2,1)}), bf16[256,2880]{0,1:T(8,128)(2,1)}) %all-reduce.2.cloned.1.call-update) | async-done | bytes 1474576 | tf_op jit(solution)/shard_map/psum | solution.py:71
  115.1 0.0 copy-done
  115.1 2.0 %fusion.6 = (f32[256]{0:T(256)S(1)}, bf16[256,2880]{0,1:T(8,128)(2,1)S(1)}) fusion(bf16[256,2880]{0,1:T(8,128)(2,1)} %all-reduce.2.cloned.1.call-done, bf16[256,2880]{0,1:T(8,128)(2,1)S(1)} %copy-done), kind=kLoop, calls=%fused_computation.17 | loop fusion | flops 5160704 | bytes 4424704 | tf_op jit(solution)/shard_map/reduce_sum | solution.py:13
  117.2 0.0 copy-done.1
  117.2 5.6 %fusion.23 = f32[256,1024]{1,0:T(8,128)} fusion(bf16[2880,1024]{1,0:T(8,128)(2,1)} %param.15, bf16[256,2880]{0,1:T(8,128)(2,1)S(1)} %get-tuple-element.18, f32[2880]{0:T(1024)S(1)} %copy-done.1, f32[256]{0:T(256)S(1)} %add_rsqrt_fusion), kind=kOutput, calls=%fused_computation.33 | convolution fusion | flops 1512898560 | bytes 8433920 | tf_op jit(solution)/shard_map/dot_general | solution.py:77
  122.7 8.3 %convolution_convert_fusion.1 = bf16[256,2880]{0,1:T(8,128)(2,1)S(1)} fusion(bf16[1024,2880]{0,1:T(8,128)(2,1)} %param.17, bf16[2880,1024]{1,0:T(8,128)(2,1)} %param.16, f32[256,1024]{1,0:T(8,128)} %fusion.23, bf16[256,2880]{0,1:T(8,128)(2,1)S(1)} %get-tuple-element.18, f32[2880]{0:T(1024)S(1)} %copy-done.1, f32[256]{0:T(256)S(1)} %add_rsqrt_fusion), kind=kOutput, calls=%fused_computation.13 | convolution fusion | flops 3025158144 | bytes 15806720 | tf_op jit(solution)/shard_map/dot_general | solution.py:84
  131.1 1.7 %copy.25 = bf16[256,2880]{1,0:T(8,128)(2,1)} copy(bf16[256,2880]{0,1:T(8,128)(2,1)S(1)} %convolution_convert_fusion.1) | data formatting | bytes 2949120
  132.8 0.0 reduce-scatter.4.cloned.1.call-update
  132.8 25.6 %reduce-scatter.4.cloned.1.call-done = bf16[128,2880]{1,0:T(8,128)(2,1)} async-done(((bf16[256,2880]{1,0:T(8,128)(2,1)}), bf16[128,2880]{1,0:T(8,128)(2,1)}) %reduce-scatter.4.cloned.1.call-update) | async-done | bytes 737296
  158.4 1.5 copy.26
  159.9 1.1 add_convert_fusion
  (3 shorter events, 0.0 us)
Async XLA Ops:
  6.5 31.1 %all-gather.2.cloned.1.call-start = ((), (), s32[]{:S(2)}) async-start(), calls=%async_computation.1 | async-start | bytes 2211840 | tf_op jit(solution)/shard_map/all_gather | solution.py:66
  7.3 107.9 %all-reduce.2.cloned.1.call-start = ((), (), s32[]{:S(2)}) async-start(), calls=%async_computation.2 | async-start | bytes 2949120 | tf_op jit(solution)/shard_map/psum | solution.py:71
  51.4 9.5 %slice-start = ((s8[11796480]{0:T(1024)(128)(4,1)}), s8[3407872]{0:T(1024)(128)(4,1)S(1)}, s32[]{:S(2)}) async-start(s8[11796480]{0:T(1024)(128)(4,1)} %bitcast.40), calls=%async_computation.4 | async-start | bytes 6815744
  51.4 9.5 %slice-start.1 = ((s8[11796480]{0:T(1024)(128)(4,1)}), s8[4194304]{0:T(1024)(128)(4,1)S(1)}, s32[]{:S(2)}) async-start(s8[11796480]{0:T(1024)(128)(4,1)} %bitcast.40), calls=%async_computation.5 | async-start | bytes 8388608
  56.5 4.7 %slice-start.2 = ((s8[11796480]{0:T(1024)(128)(4,1)}), s8[4194304]{0:T(1024)(128)(4,1)S(1)}, s32[]{:S(2)}) async-start(s8[11796480]{0:T(1024)(128)(4,1)} %bitcast.40), calls=%async_computation.6 | async-start | bytes 8388608
  61.2 53.9 %copy-start = (bf16[256,2880]{0,1:T(8,128)(2,1)S(1)}, bf16[256,2880]{0,1:T(8,128)(2,1)}, u32[]{:S(2)}) copy-start(bf16[256,2880]{0,1:T(8,128)(2,1)} %all-gather.2.cloned.1.call-done) | copy-start | bytes 4423684
  65.6 51.6 %copy-start.1 = (f32[2880]{0:T(1024)S(1)}, f32[2880]{0:T(1024)}, u32[]{:S(2)}) copy-start(f32[2880]{0:T(1024)} %param.14) | copy-start | bytes 34564
  65.6 92.8 %reduce-scatter.4.cloned.1.call-start = ((), (), s32[]{:S(2)}) async-start(), calls=%async_computation.3 | async-start | bytes 2260992
Sparse Core Ops, SparseCore 0:
  8.9 28.7 all-gather.1
  65.7 49.3 all-reduce.1
  132.9 25.4 reduce-scatter.3
where the time goes:
time: 168 us; the launch traced here: 167 us
  waiting for transfers between devices  105 us (62%)
  matrix products  33.9 us (20%)
  between operations  13.2 us (8%)
  other arithmetic  10.8 us (6%)
  local copies, waits for them, and re-layouts  4.19 us (2%)
    psum x1, waiting for transfers between devices, shards(): lax.psum(jnp.dot(mixed_heads, out_weight, preferred_element_type=jnp.floa...  49.3 us
    all_gather x1, waiting for transfers between devices, shards(): whole_rows = lax.all_gather(activations, 'tensor', axis=0, tiled=True)  29.5 us
    unnamed x4, waiting for transfers between devices  26.3 us
    dot_general x1, matrix products, shards(): jnp.dot(normalize(whole_rows, attn_gain), qkv_weight, preferred_element_t...  10 us
    dot_general x1, matrix products, shards(): jnp.dot(hidden, down_weight, preferred_element_type=jnp.float32)  8.33 us
    dot_general x1, matrix products, shards(): jnp.dot(shard_rows, gate_weight, preferred_element_type=jnp.float32)  5.56 us
    sub x1, other arithmetic, one_block(): weights = jnp.exp(scores - row_max)  5.08 us
    dot_general x1, matrix products, one_block(): jnp.einsum('ngst,tnd->sngd', softmax_out, value_rows, preferred_element_t...  4.38 us
  transfers between devices with their start and end apart: 3, of which 3 were waited for; matrix products, arithmetic and copies ran while one was open for 1% of the time, Pallas kernels for 0%

commit v1 on v0

--- a/solution.py
+++ b/solution.py
@@ -68,9 +68,14 @@
         normalize(whole_rows, attn_gain), qkv_weight, preferred_element_type=jnp.float32
     ).astype(jnp.bfloat16)
     mixed_heads = attend(projected, segment_ids)
-    head_total = lax.psum(
-        jnp.dot(mixed_heads, out_weight, preferred_element_type=jnp.float32).astype(jnp.bfloat16),
-        "tensor",
+    head_total = jnp.sum(
+        lax.all_gather(
+            jnp.dot(mixed_heads, out_weight, preferred_element_type=jnp.float32).astype(
+                jnp.bfloat16
+            ),
+            "tensor",
+        ),
+        axis=0,
     ).astype(jnp.float32)
     resid_whole = (whole_rows.astype(jnp.float32) + head_total).astype(jnp.bfloat16)
     shard_rows = normalize(resid_whole, ffn_gain)

time: 168 us -> 182 us (1.083)
  other arithmetic: 10.8 us -> 24.5 us
  local copies, waits for them, and re-layouts: 4.19 us -> 12.3 us
  waiting for transfers between devices: 105 us -> 98.4 us
    psum x1 -> x0, waiting for transfers between devices: 49.3 us -> none  [shards(): lax.psum(jnp.dot(mixed_heads, out_weight, preferred_element_type=jnp.floa...]
    all_gather x0 -> x1, waiting for transfers between devices: none -> 42.6 us  [shards(): lax.all_gather(jnp.dot(mixed_heads, out_weight, preferred_element_type=jn...]
    reduce_sum x0 -> x1, other arithmetic: none -> 15.1 us  [shards(): jnp.sum(lax.all_gather(jnp.dot(mixed_heads, out_weight, preferred_element...]
    all_gather x0 -> x1, local copies, waits for them, and re-layouts: none -> 7.04 us  [shards(): lax.all_gather(jnp.dot(mixed_heads, out_weight, preferred_element_type=jn...]
    unnamed x12 -> x16, local copies, waits for them, and re-layouts: 3.57 us -> 4.69 us
  transfers between devices with their start and end apart: 3 -> 3, of which waited for: 3 -> 3; matrix products, arithmetic and copies ran while one was open for 1% -> 0% of each run, Pallas kernels for 0% -> 0%
where the time goes in v1:
time: 182 us
  waiting for transfers between devices  98.4 us (54%)
  matrix products  33.1 us (18%)
  other arithmetic  24.5 us (13%)
  between operations  13.2 us (7%)
  local copies, waits for them, and re-layouts  12.3 us (7%)
    all_gather x1, waiting for transfers between devices, shards(): lax.all_gather(jnp.dot(mixed_heads, out_weight, preferred_element_type=jn...  42.6 us
    all_gather x1, waiting for transfers between devices, shards(): whole_rows = lax.all_gather(activations, 'tensor', axis=0, tiled=True)  29.5 us
    unnamed x4, waiting for transfers between devices  26.3 us
    reduce_sum x1, other arithmetic, shards(): jnp.sum(lax.all_gather(jnp.dot(mixed_heads, out_weight, preferred_element...  15.1 us
    dot_general x1, matrix products, shards(): jnp.dot(normalize(whole_rows, attn_gain), qkv_weight, preferred_element_t...  10 us
    dot_general x1, matrix products, shards(): jnp.dot(hidden, down_weight, preferred_element_type=jnp.float32)  8.5 us
    all_gather x1, local copies, waits for them, and re-layouts, shards(): lax.all_gather(jnp.dot(mixed_heads, out_weight, preferred_element_type=jn...  7.04 us
    sub x1, other arithmetic, one_block(): weights = jnp.exp(scores - row_max)  5.08 us
  transfers between devices with their start and end apart: 3, of which 3 were waited for; matrix products, arithmetic and copies ran while one was open for 0% of the time, Pallas kernels for 0%

profile of v1, /device:TPU:0, one launch (start us, length us, event | category | flops | bytes accessed | tf_op | source)
XLA Modules:
  0.0 181.9 jit_solution(12478699107135717071)
XLA Ops:
  6.5 0.0 all-gather.4.cloned.1.call-start
  6.5 0.7 all-gather.4.cloned.1.call-update
  7.3 0.0 all-gather.6.cloned.1.call-start
  7.3 0.9 fusion.25
  8.2 29.5 %all-gather.4.cloned.1.call-done = bf16[256,2880]{0,1:T(8,128)(2,1)} async-done(((bf16[128,2880]{0,1:T(8,128)(2,1)}), bf16[256,2880]{0,1:T(8,128)(2,1)}) %all-gather.4.cloned.1.call-update) | async-done | bytes 1474576 | tf_op jit(solution)/shard_map/all_gather | solution.py:66
  37.7 1.8 fusion.9
  39.5 10.0 %convolution_convert_fusion.2 = bf16[256,2560]{1,0:T(8,128)(2,1)S(1)} fusion(bf16[2880,2560]{1,0:T(8,128)(2,1)} %param.12, bf16[256,2880]{0,1:T(8,128)(2,1)} %all-gather.4.cloned.1.call-done, f32[2880]{0:T(1024)} %param.11, f32[256]{0:T(256)S(1)} %add_rsqrt_fusion.1), kind=kOutput, calls=%fused_computation.14 | convolution fusion | flops 3778478080 | bytes 17543424 | tf_op jit(solution)/shard_map/dot_general | solution.py:67
  49.5 0.6 copy.18
  50.1 1.3 fusion.18
  51.4 0.0 slice-start
  51.4 0.0 slice-start.1
  51.4 5.1 %fusion.30 = (f32[4,8,256]{2,1,0:T(8,128)S(1)}, f32[4,8,256,256]{2,3,1,0:T(8,128)}) fusion(f32[4,256,256,8]{2,1,3,0:T(8,128)S(1)} %fusion.18, pred[256,256]{0,1:T(8,128)(4,1)S(1)} %fusion.25), kind=kOutput, calls=%fused_computation.43 | output fusion | flops 12583167 | bytes 16875520 | tf_op jit(solution)/shard_map/while/body/eval_jaxpr/sub | solution.py:42
  56.5 0.0 slice-start.2
  56.5 4.4 %fusion.13 = bf16[4,64,8,256]{3,1,2,0:T(8,128)(2,1)S(1)} fusion(f32[4,8,256,256]{2,3,1,0:T(8,128)} %get-tuple-element.20, f32[4,8,256]{2,1,0:T(8,128)S(1)} %get-tuple-element.19, bf16[256,4,10,64]{0,3,2,1:T(8,128)(2,1)S(1)} %bitcast.41), kind=kOutput, calls=%fused_computation.24 | convolution fusion | flops 273154048 | bytes 9601024 | tf_op jit(solution)/shard_map/while/body/eval_jaxpr/ngst,tnd->sngd/dot_general | solution.py:45
  60.9 0.0 slice-done
  60.9 0.0 slice-done.1
  60.9 0.3 slice-done.2
  61.2 4.4 %convolution_convert_fusion = bf16[256,2880]{0,1:T(8,128)(2,1)} fusion(bf16[2048,2880]{0,1:T(8,128)(2,1)S(1)} %bitcast.43, bf16[256,2048]{0,1:T(8,128)(2,1)S(1)} %bitcast.44), kind=kOutput, calls=%fused_computation.12 | convolution fusion | flops 3020636160 | bytes 14319616 | tf_op jit(solution)/shard_map/dot_general | solution.py:73
  65.6 0.0 all-gather.6.cloned.1.call-update
  65.6 0.2 reduce-scatter.4.cloned.1.call-start
  65.8 42.6 %all-gather.6.cloned.1.call-done = bf16[512,2880]{0,1:T(8,128)(2,1)} async-done(((bf16[256,2880]{0,1:T(8,128)(2,1)}), bf16[512,2880]{0,1:T(8,128)(2,1)}) %all-gather.6.cloned.1.call-update) | async-done | bytes 2949136 | tf_op jit(solution)/shard_map/all_gather | solution.py:72
  108.4 7.0 %reshape.32 = bf16[2,256,2880]{1,0,2:T(2,128)(2,1)} reshape(bf16[512,2880]{0,1:T(8,128)(2,1)} %all-gather.6.cloned.1.call-done) | data formatting | bytes 5898240 | tf_op jit(solution)/shard_map/all_gather | solution.py:72
  115.5 0.0 copy-start
  115.5 15.1 %reduce_sum.42 = bf16[256,2880]{0,1:T(8,128)(2,1)S(1)} reduce(bf16[2,256,2880]{1,0,2:T(2,128)(2,1)} %reshape.32, bf16[]{:T(256)} %constant.42.clone.1), dimensions={0}, to_apply=%region_3.4 | reduce | flops 737280 | bytes 4423682 | tf_op jit(solution)/shard_map/reduce_sum | solution.py:71
  130.6 0.0 copy-done
  130.6 0.0 copy-start.3
  130.6 0.6 fusion.6
  131.2 0.0 copy-start.1
  131.3 1.1 copy-done.1
  132.4 0.0 copy-done.3
  132.4 4.6 %fusion.23 = f32[256,1024]{1,0:T(8,128)S(1)} fusion(bf16[2880,1024]{1,0:T(8,128)(2,1)} %param.15, bf16[256,2880]{0,1:T(8,128)(2,1)S(1)} %get-tuple-element.18, f32[2880]{0:T(1024)S(1)} %copy-done.3, f32[256]{0:T(256)S(1)} %add_rsqrt_fusion), kind=kOutput, calls=%fused_computation.33 | convolution fusion | flops 1512898560 | bytes 8433920 | tf_op jit(solution)/shard_map/dot_general | solution.py:82
  137.0 8.5 %convolution_convert_fusion.1 = bf16[256,2880]{0,1:T(8,128)(2,1)S(1)} fusion(bf16[1024,2880]{0,1:T(8,128)(2,1)} %param.17, bf16[2880,1024]{1,0:T(8,128)(2,1)} %param.16, f32[256,1024]{1,0:T(8,128)S(1)} %fusion.23, bf16[256,2880]{0,1:T(8,128)(2,1)} %copy-done.1, f32[2880]{0:T(1024)S(1)} %copy-done.3, f32[256]{0:T(256)S(1)} %add_rsqrt_fusion), kind=kOutput, calls=%fused_computation.13 | convolution fusion | flops 3025158144 | bytes 15806720 | tf_op jit(solution)/shard_map/dot_general | solution.py:89
  145.5 0.0 copy-start.2
  145.5 1.7 copy.25
  147.2 0.0 reduce-scatter.4.cloned.1.call-update
  147.2 25.6 %reduce-scatter.4.cloned.1.call-done = bf16[128,2880]{1,0:T(8,128)(2,1)} async-done(((bf16[256,2880]{1,0:T(8,128)(2,1)}), bf16[128,2880]{1,0:T(8,128)(2,1)}) %reduce-scatter.4.cloned.1.call-update) | async-done | bytes 737296
  172.8 1.5 copy.26
  174.3 0.0 copy-done.2
  174.3 1.1 add_convert_fusion
  (3 shorter events, 0.0 us)
Async XLA Ops:
  6.5 31.1 %all-gather.4.cloned.1.call-start = ((), (), s32[]{:S(2)}) async-start(), calls=%async_computation.1 | async-start | bytes 2211840 | tf_op jit(solution)/shard_map/all_gather | solution.py:66
  7.3 101.2 %all-gather.6.cloned.1.call-start = ((), (), s32[]{:S(2)}) async-start(), calls=%async_computation.2 | async-start | bytes 4423680 | tf_op jit(solution)/shard_map/all_gather | solution.py:72
  51.4 9.5 %slice-start = ((s8[11796480]{0:T(1024)(128)(4,1)}), s8[3407872]{0:T(1024)(128)(4,1)S(1)}, s32[]{:S(2)}) async-start(s8[11796480]{0:T(1024)(128)(4,1)} %bitcast.42), calls=%async_computation.4 | async-start | bytes 6815744
  51.4 9.5 %slice-start.1 = ((s8[11796480]{0:T(1024)(128)(4,1)}), s8[4194304]{0:T(1024)(128)(4,1)S(1)}, s32[]{:S(2)}) async-start(s8[11796480]{0:T(1024)(128)(4,1)} %bitcast.42), calls=%async_computation.5 | async-start | bytes 8388608
  56.5 4.7 %slice-start.2 = ((s8[11796480]{0:T(1024)(128)(4,1)}), s8[4194304]{0:T(1024)(128)(4,1)S(1)}, s32[]{:S(2)}) async-start(s8[11796480]{0:T(1024)(128)(4,1)} %bitcast.42), calls=%async_computation.6 | async-start | bytes 8388608
  65.6 107.2 %reduce-scatter.4.cloned.1.call-start = ((), (), s32[]{:S(2)}) async-start(), calls=%async_computation.3 | async-start | bytes 2260992
  115.5 15.1 %copy-start = (bf16[256,2880]{0,1:T(8,128)(2,1)S(1)}, bf16[256,2880]{0,1:T(8,128)(2,1)}, u32[]{:S(2)}) copy-start(bf16[256,2880]{0,1:T(8,128)(2,1)} %all-gather.4.cloned.1.call-done) | copy-start | bytes 4423684
  130.6 1.8 copy-start.3
  131.2 1.1 copy-start.1
  145.5 28.8 %copy-start.2 = (bf16[256,2880]{0,1:T(8,128)(2,1)S(1)}, bf16[256,2880]{0,1:T(8,128)(2,1)}, u32[]{:S(2)}) copy-start(bf16[256,2880]{0,1:T(8,128)(2,1)} %copy-done.1) | copy-start | bytes 4423684
Sparse Core Ops, SparseCore 0:
  8.9 28.7 all-gather.3
  65.7 42.6 all-gather.5
  147.4 25.4 reduce-scatter.3
